TPU v7x, 128 devices: a whole 4x4x4 slice. The times are simulated.
128 devices in a mesh: gx: 8 (over x, core), gy: 16 (over y, z).
Axes of the slice: x: 4, y: 4, z: 4, core: 2. Of those that a mesh axis runs over, the one named last changes fastest.
Arguments:
- log_crit: float32 [1024, 1024, 128], P('gx', 'gy'), may hold values from -4 to 4
- col_bins: int32 [1024, 1024, 4], P('gx', 'gy'), may hold values from 0 to 127
- rate_table: bfloat16 [128, 64], replicated, may hold values from 0.0039978027 to 0.059814453
- tile_mask: int32 [32, 32, 4], P('gx', 'gy'), may hold values from 0 to 1, as said below
- tile_route: int32 [32, 32, 4], P('gx', 'gy'), may hold values from 0 to 15, as said below
- filt_x: float32 [1024], replicated, may hold values from 0.1 to 1, as said below
- filt_y: float32 [1024], replicated, may hold values from 0.1 to 1, as said below
Outputs:
- recomb: float32 [1024, 1024, 128], P('gx', 'gy')
- smoothed: float32 [1024, 1024, 128], P('gx', 'gy')
- load: float32 [8, 16], P('gx', 'gy')
Inputs may be any that keep to these rules, and one draw needn't show every extreme that they name: `tile_mask`: tiles form blocks of 4 x 2 x 4 (indices a // 4, b // 2); among the blocks with the same a // 4, some block has all 32 tiles active. `tile_route`: counting only tiles with tile_mask 1: among the blocks with the same a // 4 at most 16 active tiles share a route, and in every draw some such row of blocks gives every route exactly 16; at most 2 active tiles of one block share a route, and in every draw some block has 2 that do. filt_x[m] == filt_x[1024 - m] for 0 < m < 1024. filt_y[n] == filt_y[1024 - n] for 0 < n < 1024.
All inputs are finite; a program needn't handle non-finite values.
Results may differ from a plain program's by a relative error of at most 0.0003.
Values sent between devices are 32-bit elements; how exact they have to be, the bound alone decides.
A program may use at most 128 MiB of HBM per device.

v0:
```python
import functools
import math

import jax
import jax.numpy as jnp
import numpy as np
from jax import lax
from jax.experimental import pallas as pl
from jax.experimental.pallas import tpu as pltpu
from jax.sharding import PartitionSpec as P

VMEM = pltpu.VMEM


def pair_constants(nodes):
    half = nodes // 2
    q = -2.5 + 5.0 * np.arange(half) / (nodes - 1)
    g = np.exp(3.0 * q)
    return g, g + 1.0 / g


def pair_table(rate_table):
    nodes = rate_table.shape[1]
    g, _ = pair_constants(nodes)
    table = rate_table.astype(jnp.float32).T
    a = table[: nodes // 2]
    b = table[nodes // 2 :][::-1]
    g = jnp.asarray(g[:, None], jnp.float32)
    return jnp.concatenate([a + b, a / g + b * g], axis=0)


def column_integral(field, index_row, table_ref, coef_ref, sums):
    nodes = table_ref.shape[0]
    half = nodes // 2
    _, s = pair_constants(nodes)
    index = jnp.broadcast_to(index_row, (8, 128))
    for part in range(nodes // 8):
        rows = pl.ds(8 * part, 8)
        coef_ref[rows, :] = jnp.take_along_axis(
            table_ref[rows, :], index, axis=1, mode="promise_in_bounds"
        )
    w = jnp.exp(3.0 * field)
    v = w + jnp.exp(-3.0 * field)
    total = jnp.zeros_like(field)
    for k in range(half):
        r = pl.reciprocal(v + np.float32(s[k]), approx=False)
        total = total + (w * coef_ref[k : k + 1, :] + coef_ref[half + k : half + k + 1, :]) * r
    return total


def kernel_rows(filt):
    size = filt.shape[0]
    inner = 32
    outer = size // inner
    a = np.arange(outer)[:, None] * np.arange(outer)[None, :]
    small = 2.0 * np.pi * (a % outer) / outer
    b = np.arange(inner)[:, None] * np.arange(size)[None, :]
    big = 2.0 * np.pi * (b % size) / size
    grid = filt.reshape(outer, inner)
    dot = functools.partial(jnp.einsum, precision=lax.Precision.HIGHEST)
    real = dot("ab,ar->br", grid, jnp.asarray(np.cos(small), jnp.float32))
    imag = dot("ab,ar->br", grid, jnp.asarray(np.sin(small), jnp.float32))
    real = jnp.tile(real, (1, size // outer))
    imag = jnp.tile(imag, (1, size // outer))
    c = jnp.sum(
        real * jnp.asarray(np.cos(big), jnp.float32) - imag * jnp.asarray(np.sin(big), jnp.float32),
        axis=0,
    )
    return (c / size).reshape(size // 128, 128)


def split(x):
    high = x.astype(jnp.bfloat16)
    return high, (x - high.astype(jnp.float32)).astype(jnp.bfloat16)


def build_circulants(c_ref, mat_ref):
    shift = lax.rem(
        lax.broadcasted_iota(jnp.int32, (128, 128), 1)
        - lax.broadcasted_iota(jnp.int32, (128, 128), 0)
        + 128,
        128,
    )
    upper = lax.broadcasted_iota(jnp.int32, (128, 128), 1) >= lax.broadcasted_iota(
        jnp.int32, (128, 128), 0
    )
    rolled = []
    for m in range(8):
        row = jnp.broadcast_to(c_ref[m : m + 1, :], (8, 128))
        rolled.append(
            jnp.concatenate(
                [
                    jnp.take_along_axis(row, shift[8 * g : 8 * g + 8], axis=1, mode="promise_in_bounds")
                    for g in range(16)
                ],
                axis=0,
            )
        )
    blocks = [jnp.where(upper, rolled[(-d) % 8], rolled[(-d - 1) % 8]) for d in range(8)]
    for d in range(-3, 4):
        near, far = blocks[d % 8], blocks[(d + 4) % 8]
        for sign, value in enumerate((0.5 * (near + far), 0.5 * (near - far))):
            for part, piece in enumerate(split(value)):
                for i in range(4):
                    j = i - d
                    if 0 <= j < 4:
                        mat_ref[sign, part, pl.ds(128 * i, 128), pl.ds(128 * j, 128)] = piece


def dot3(a, b):
    d = functools.partial(jnp.dot, preferred_element_type=jnp.float32)
    return d(a[0], b[0]) + d(a[0], b[1]) + d(a[1], b[0])


MESH = pl.DeviceIdType.MESH


def fused_kernel(
    field_hbm, bins_ref, table_ref, mask_ref, route_ref, cx_ref, cy_ref,
    recomb_hbm, back_ref, share_ref,
    field_buf, out_buf, zsend_ref, recv_ref, mx_ref, my_ref, mid_ref, send_ref, give_ref,
    coef_ref, lt_ref, rt_ref, sum_ref,
    in_sem, out_sem, fsend_sem, frecv_sem, bsend_sem, brecv_sem, lsend_sem, lrecv_sem,
):
    n_gx, n_gy = lax.axis_size("gx"), lax.axis_size("gy")
    total = n_gx * n_gy
    gx, gy = lax.axis_index("gx"), lax.axis_index("gy")
    me = gx * n_gy + gy
    edge = 32
    layers = bins_ref.shape[1]
    chunks = zsend_ref.shape[0]
    pieces = send_ref.shape[0]
    piece_rows = send_ref.shape[2]

    def peer(k):
        offset = lax.rem(k * 37, total)
        return lax.rem(gx + offset // n_gy, n_gx), lax.rem(gy + lax.rem(offset, n_gy), n_gy)

    def forward(c, k):
        tx, ty = peer(k)
        return pltpu.make_async_remote_copy(
            src_ref=zsend_ref.at[c, tx * n_gy + ty], dst_ref=recv_ref.at[c, me],
            send_sem=fsend_sem.at[c], recv_sem=frecv_sem.at[c],
            device_id=(tx, ty), device_id_type=MESH,
        )

    def backward(p, k):
        tx, ty = peer(k)
        rows = pl.ds(pl.multiple_of(p * piece_rows, piece_rows), piece_rows)
        return pltpu.make_async_remote_copy(
            src_ref=send_ref.at[p, tx * n_gy + ty], dst_ref=back_ref.at[me, rows],
            send_sem=bsend_sem.at[p], recv_sem=brecv_sem.at[p],
            device_id=(tx, ty), device_id_type=MESH,
        )

    def load_copy(k):
        ty = lax.rem(gy + k, n_gy)
        return pltpu.make_async_remote_copy(
            src_ref=give_ref.at[ty], dst_ref=share_ref.at[gy],
            send_sem=lsend_sem, recv_sem=lrecv_sem,
            device_id=(gx, ty), device_id_type=MESH,
        )

    def fetch(c, slot):
        return pltpu.make_async_copy(
            field_hbm.at[:, pl.ds(pl.multiple_of(c * 8, 8), 8), :], field_buf.at[slot], in_sem.at[slot]
        )

    def put(c, slot):
        return pltpu.make_async_copy(
            out_buf.at[slot], recomb_hbm.at[:, pl.ds(pl.multiple_of(c * 8, 8), 8), :], out_sem.at[slot]
        )

    fetch(0, 0).start()
    barrier = pltpu.get_barrier_semaphore()

    def greet(k, _):
        tx, ty = peer(k)
        pl.semaphore_signal(barrier, inc=1, device_id=(tx, ty), device_id_type=MESH)
        return 0

    lax.fori_loop(1, total, greet, 0)
    sum_ref[...] = jnp.zeros_like(sum_ref)

    def evaluate_chunk(c, sending):
        slot = lax.rem(c, 2)

        @pl.when(c + 1 < chunks)
        def _():
            fetch(c + 1, 1 - slot).start()

        fetch(c, slot).wait()

        @pl.when(c >= 2)
        def _():
            put(c - 2, slot).wait()

        field2 = field_buf.at[slot].reshape(128 * 8, 128)
        out2 = out_buf.at[slot].reshape(128 * 8, 128)
        zsend2 = zsend_ref.at[c].reshape(128 * 8, 128)
        band = c * 8 // edge

        def per_row(y, _):
            lt_ref[...] = field2[pl.ds(y, 128, stride=8), :].T
            for t in range(layers):
                if sending:
                    per = total // 8 // layers
                    for s in range(per):
                        k = (y * layers + t) * per + s + 1
                        if t == layers - 1 and s == per - 1:
                            @pl.when(k < total)
                            def _():
                                forward(c - 1, k).start()
                        else:
                            forward(c - 1, k).start()
                z = pl.ds(edge * t, edge)
                value = column_integral(lt_ref[z, :], bins_ref[c * 8 + y, t : t + 1, :], table_ref, coef_ref, None)
                value = value * mask_ref[pl.ds(band * layers + t, 1), :]
                rt_ref[z, :] = value
                folded = (value[0:8] + value[8:16]) + (value[16:24] + value[24:32])
                sum_ref[band * layers + t] += folded
            zsend2[pl.ds(y, 128, stride=8), :] = rt_ref[...]
            out2[pl.ds(y, 128, stride=8), :] = rt_ref[...].T
            return 0

        lax.fori_loop(0, 8, per_row, 0)
        recv_ref[c, me] = zsend_ref[c, me]
        put(c, slot).start()

    evaluate_chunk(0, False)
    pl.semaphore_wait(barrier, total - 1)

    def later_chunk(c, _):
        evaluate_chunk(c, True)
        return 0

    lax.fori_loop(1, chunks, later_chunk, 0)

    def last_send(k, _):
        forward(chunks - 1, k).start()
        return 0

    lax.fori_loop(1, total, last_send, 0)

    flat = jnp.concatenate(
        [jnp.sum(sum_ref[i], axis=0, keepdims=True) for i in range(8)], axis=0
    )
    for g in range(16):
        give_ref[g] = jnp.where(route_ref[...] == g, flat, 0.0)
    share_ref[gy] = give_ref[gy]

    build_circulants(cx_ref, mx_ref)
    build_circulants(cy_ref, my_ref)

    def load_send(k, _):
        load_copy(k).start()
        return 0

    lax.fori_loop(1, n_gy, load_send, 0)

    def wait_all(ref, send_sem, recv_sem, what):
        copy = pltpu.make_async_remote_copy(
            src_ref=ref, dst_ref=ref, send_sem=send_sem, recv_sem=recv_sem,
            device_id=(gx, gy), device_id_type=MESH,
        )
        copy.wait_recv() if what == "recv" else copy.wait_send()

    def first(c, _):
        for q in range(2):
            wait_all(recv_ref.at[2 * c + q, pl.ds(0, total - 1)], fsend_sem.at[2 * c + q], frecv_sem.at[2 * c + q], "recv")

        def rows(i, j0):
            src = pl.ds(i * 16 + j0, 8)
            return jnp.concatenate([recv_ref[2 * c, src], recv_ref[2 * c + 1, src]], axis=1).reshape(128, 128)

        for ysign in range(2):
            parts = [[], []]
            for i in range(4):
                a0, a1 = rows(i, 0), rows(i, 8)
                b0, b1 = rows(i + 4, 0), rows(i + 4, 8)
                if ysign == 0:
                    a, b = a0 + a1, b0 + b1
                else:
                    a, b = a0 - a1, b0 - b1
                parts[0].append(a + b)
                parts[1].append(a - b)
            for xsign in range(2):
                value = split(jnp.concatenate(parts[xsign], axis=1))
                out = split(dot3(value, (mx_ref[xsign, 0], mx_ref[xsign, 1])))
                for part in range(2):
                    for j in range(8):
                        mid_ref[ysign, part, pl.ds(pl.multiple_of(64 * j + 16 * c, 16), 16), pl.ds(512 * xsign, 512)] = out[part][16 * j : 16 * j + 16]
        return 0

    lax.fori_loop(0, chunks // 2, first, 0)

    def second(p, _):
        res = []
        for ysign in range(2):
            mat = [
                jnp.concatenate(
                    [my_ref[ysign, part, pl.ds(pl.multiple_of(64 * j + 16 * p, 16), 16), :] for j in range(8)],
                    axis=0,
                )
                for part in range(2)
            ]
            res.append(dot3(mat, (mid_ref[ysign, 0], mid_ref[ysign, 1])))
        for yh in range(2):
            both = res[0] + res[1] if yh == 0 else res[0] - res[1]
            plus, minus = both[:, :512], both[:, 512:]
            for xh in range(2):
                value = plus + minus if xh == 0 else plus - minus
                for i in range(4):
                    for j in range(8):
                        send_ref[p, (xh * 4 + i) * 16 + yh * 8 + j] = value[16 * j : 16 * j + 16, 128 * i : 128 * i + 128]
        back_ref[me, pl.ds(pl.multiple_of(p * piece_rows, piece_rows), piece_rows)] = send_ref[p, me]

        def send(k, _):
            backward(p, k).start()
            return 0

        lax.fori_loop(1, total, send, 0)
        return 0

    lax.fori_loop(0, pieces, second, 0)

    def finish_forward(c, _):
        wait_all(zsend_ref.at[c, pl.ds(0, total - 1)], fsend_sem.at[c], frecv_sem.at[c], "send")
        return 0

    lax.fori_loop(0, chunks, finish_forward, 0)
    wait_all(share_ref.at[pl.ds(0, n_gy - 1)], lsend_sem, lrecv_sem, "recv")
    wait_all(give_ref.at[pl.ds(0, n_gy - 1)], lsend_sem, lrecv_sem, "send")
    put(chunks - 2, 0).wait()
    put(chunks - 1, 1).wait()

    def finish_backward(p, _):
        rows = pl.ds(pl.multiple_of(p * piece_rows, piece_rows), piece_rows)
        wait_all(back_ref.at[pl.ds(0, total - 1), rows], bsend_sem.at[p], brecv_sem.at[p], "recv")
        wait_all(send_ref.at[p, pl.ds(0, total - 1)], bsend_sem.at[p], brecv_sem.at[p], "send")
        return 0

    lax.fori_loop(0, pieces, finish_backward, 0)


def fused_call(log_crit, bins, table, mask_rows, route_rows, cx, cy):
    f32, bf16 = jnp.float32, jnp.bfloat16
    cells_x, cells_y, depth = log_crit.shape
    total = 128
    chunks, pieces = 8, 4
    dma, vmem, anywhere = pltpu.SemaphoreType.DMA, pl.BlockSpec(memory_space=VMEM), pl.BlockSpec(memory_space=pl.ANY)
    return pl.pallas_call(
        fused_kernel,
        in_specs=[anywhere] + [vmem] * 6,
        out_specs=[anywhere, vmem, vmem],
        out_shape=[
            jax.ShapeDtypeStruct((cells_x, cells_y, depth), f32),
            jax.ShapeDtypeStruct((total, cells_y, cells_x), f32),
            jax.ShapeDtypeStruct((16, 8, 128), f32),
        ],
        scratch_shapes=[
            VMEM((2, cells_x, 8, depth), f32),
            VMEM((2, cells_x, 8, depth), f32),
            VMEM((chunks, total, 8, 128), f32),
            VMEM((chunks, total, 8, 128), f32),
            VMEM((2, 2, 512, 512), bf16),
            VMEM((2, 2, 512, 512), bf16),
            VMEM((2, 2, 512, 1024), bf16),
            VMEM((pieces, total, 64 // pieces, 128), f32),
            VMEM((16, 8, 128), f32),
            VMEM(table.shape, f32),
            VMEM((128, 128), f32),
            VMEM((128, 128), f32),
            VMEM((8, 8, 128), f32),
            dma((2,)), dma((2,)), dma((chunks,)), dma((chunks,)), dma((pieces,)), dma((pieces,)), dma, dma,
        ],
        compiler_params=pltpu.CompilerParams(
            vmem_limit_bytes=60 * 2**20, collective_id=0, has_side_effects=True
        ),
        name="fused",
    )(log_crit, bins, table, mask_rows, route_rows, cx, cy)


def final_kernel(back_ref, recomb_ref, share_ref, out_ref, recomb_out, load_ref):
    source = back_ref.reshape(128 * 8, 128)
    target = out_ref.reshape(128 * 8, 128)
    for y in range(8):
        target[pl.ds(y, 128, stride=8), :] = source[pl.ds(y, 128, stride=8), :].T
    recomb_out[...] = recomb_ref[...]
    all_shares = jnp.sum(share_ref[...], axis=0)
    load_ref[...] = jnp.sum(jnp.sum(all_shares, axis=0, keepdims=True), axis=1, keepdims=True) * (2.0**-19)


def final_call(back, recomb, share):
    depth, cells_y, cells_x = back.shape
    steps = cells_y // 8
    f32 = jnp.float32
    slab = pl.BlockSpec((cells_x // steps, cells_y, depth), lambda c: (c, 0, 0))
    return pl.pallas_call(
        final_kernel,
        grid=(steps,),
        in_specs=[
            pl.BlockSpec((depth, 8, cells_x), lambda c: (0, c, 0)),
            slab,
            pl.BlockSpec(share.shape, lambda c: (0, 0, 0)),
        ],
        out_specs=[
            pl.BlockSpec((cells_x, 8, depth), lambda c: (0, c, 0)),
            slab,
            pl.BlockSpec((1, 1), lambda c: (0, 0)),
        ],
        out_shape=[
            jax.ShapeDtypeStruct((cells_x, cells_y, depth), f32),
            jax.ShapeDtypeStruct((cells_x, cells_y, depth), f32),
            jax.ShapeDtypeStruct((1, 1), f32),
        ],
        name="final",
    )(back, recomb, share)


def on_device(log_crit, col_bins, rate_table, tile_mask, tile_route, filt_x, filt_y):
    tiles_x = tile_mask.shape[0]
    edge = log_crit.shape[0] // tiles_x
    bins = col_bins.transpose(1, 2, 0)

    def rows_of(tiles):
        return jnp.repeat(tiles.transpose(1, 2, 0).reshape(-1, tiles_x), edge, axis=1)

    mask_rows = rows_of((tile_mask == 1).astype(jnp.float32))
    recomb, back, share = fused_call(
        log_crit, bins, pair_table(rate_table), mask_rows, rows_of(tile_route),
        kernel_rows(filt_x), kernel_rows(filt_y),
    )
    smoothed, recomb, load = final_call(back, recomb, share)
    return recomb, smoothed, load


def solution(mesh):
    block = P("gx", "gy", None)
    return jax.shard_map(
        on_device,
        mesh=mesh,
        in_specs=(block, block, P(), block, block, P(), P()),
        out_specs=(block, block, P("gx", "gy")),
        check_vma=False,
    )
```

profile of v0, /device:TPU:1, one launch (start us, length us, event | category | flops | bytes accessed | tf_op | source)
XLA Modules:
  0.0 151.3 jit_solution(13705145030280022589)
XLA Ops:
  0.6 0.7 fusion
  1.3 0.1 copy.31
  1.4 0.8 copy.32
  2.2 0.1 broadcast_in_dim.7
  2.3 0.7 reshape.55.route_ref
  2.9 0.1 broadcast_in_dim.6
  3.0 0.7 reshape.53.mask_ref
  3.7 0.8 reshape.56
  4.5 0.8 reshape.57
  5.2 0.9 convolution_bitcast_fusion
  6.1 0.9 convolution_bitcast_fusion.1
  7.1 0.1 copy.29
  7.2 0.1 copy.30
  7.2 0.9 convolution_bitcast_fusion.2
  8.2 0.9 convolution_bitcast_fusion.3
  9.1 0.1 copy.27
  9.2 0.1 copy.28
  9.2 1.4 subtract_reduce_fusion
  10.7 0.7 div.26.cy_ref
  11.3 0.7 div.24.cx_ref
  12.0 0.7 convert_bitcast_fusion
  12.7 0.7 slice_add_fusion
  13.5 0.6 pad_maximum_fusion.table_ref
  14.1 127.6 %fused.1 = (f32[128,64,128]{2,1,0:T(8,128)}, f32[128,64,128]{2,1,0:T(8,128)}, f32[16,8,128]{2,1,0:T(8,128)}) custom-call(f32[128,64,128]{2,1,0:T(8,128)} %field_hbm.1, s32[64,4,128]{2,1,0:T(4,128)} %bitcast.24, f32[64,128]{1,0:T(8,128)} %pad_maximum_fusion.table_ref, f32[8,128]{1,0:T(8,128)} %reshape.53.mask_ref, s32[8,128]{1,0:T(8,128)} %reshape.55.route_ref, ...), custom_call_target="tpu_custom_call" | custom-call | tf_op jit(solution)/shard_map/fused/pallas_call | solution.py:352
  141.8 9.5 %final.1 = (f32[128,64,128]{2,1,0:T(8,128)}, f32[128,64,128]{2,1,0:T(8,128)}, f32[1,1]{1,0:T(1,128)}) custom-call(f32[128,64,128]{2,1,0:T(8,128)} %get-tuple-element.9.back_ref, f32[128,64,128]{2,1,0:T(8,128)} %get-tuple-element.10.recomb_ref, f32[16,8,128]{2,1,0:T(8,128)} %get-tuple-element.11.share_ref), custom_call_target="tpu_custom_call" | custom-call | tf_op jit(solution)/shard_map/final/pallas_call | solution.py:399
  (3 shorter events, 0.0 us)
where the time goes:
time: 152 us; the launch traced here: 151 us
  Pallas kernels  137 us (90%)
  local copies, waits for them, and re-layouts  5.52 us (4%)
  other arithmetic  4.2 us (3%)
  matrix products  3.71 us (2%)
    pallas_call x1, Pallas kernels, fused_call(): pl.pallas_call(fused_kernel, in_specs=[anywhere] + [vmem] * 6, out_specs=...  128 us
    pallas_call x1, Pallas kernels, final_call(): pl.pallas_call(final_kernel, grid=(steps,), in_specs=[pl.BlockSpec((depth...  9.5 us

commit v1 on v0

v1 whole, which is shorter than its diff:
```python
import functools

import jax
import jax.numpy as jnp
import numpy as np
from jax import lax
from jax.experimental import pallas as pl
from jax.experimental.pallas import tpu as pltpu
from jax.sharding import PartitionSpec as P

VMEM = pltpu.VMEM


MESH = pl.DeviceIdType.MESH
EDGE = 32


def pair_constants(nodes):
    half = nodes // 2
    q = -2.5 + 5.0 * np.arange(half) / (nodes - 1)
    g = np.exp(3.0 * q)
    return g, g + 1.0 / g


def wave_tables(size):
    inner = 32
    outer = size // inner
    a = np.arange(outer)[:, None] * (np.arange(128)[None, :] % outer)
    small = 2.0 * np.pi * (a % outer) / outer
    b = np.arange(inner)[:, None] * np.arange(size)[None, :]
    big = 2.0 * np.pi * (b % size) / size
    waves = [np.concatenate([f(small), f(big) / size], axis=1) for f in (np.cos, np.sin)]
    return np.concatenate(waves, axis=0).astype(np.float32)


def build_pair_table(rate_ref, wide_ref, table_ref):
    nodes = rate_ref.shape[0]
    half = nodes // 2
    g, _ = pair_constants(nodes)
    wide_ref[...] = rate_ref[...].astype(jnp.float32)
    for k in range(half):
        a = wide_ref[k : k + 1, :]
        b = wide_ref[nodes - 1 - k : nodes - k, :]
        table_ref[k : k + 1, :] = a + b
        table_ref[half + k : half + k + 1, :] = a * np.float32(1.0 / g[k]) + b * np.float32(g[k])


def build_rows(tiles_ref, rows_ref):
    tiles_x, tiles_y, tiles_z = tiles_ref.shape
    group = lax.broadcasted_iota(jnp.int32, (1, 128), 1) // EDGE
    for b in range(tiles_y):
        for t in range(tiles_z):
            row = jnp.zeros((1, 128), jnp.int32)
            for a in range(tiles_x):
                value = jnp.broadcast_to(tiles_ref[a, b : b + 1, t : t + 1], (1, 128))
                row = jnp.where(group == a, value, row)
            i = b * tiles_z + t
            rows_ref[i : i + 1, :] = row


def column_integral(field, index_row, table_ref, coef_ref):
    nodes = table_ref.shape[0]
    half = nodes // 2
    _, s = pair_constants(nodes)
    index = jnp.broadcast_to(index_row, (8, 128))
    for part in range(nodes // 8):
        rows = pl.ds(8 * part, 8)
        coef_ref[rows, :] = jnp.take_along_axis(
            table_ref[rows, :], index, axis=1, mode="promise_in_bounds"
        )
    w = jnp.exp(3.0 * field)
    v = w + jnp.exp(-3.0 * field)
    total = jnp.zeros_like(field)
    for k in range(half):
        r = pl.reciprocal(v + np.float32(s[k]), approx=False)
        total = total + (w * coef_ref[k : k + 1, :] + coef_ref[half + k : half + k + 1, :]) * r
    return total


def split(x):
    high = x.astype(jnp.bfloat16)
    return high, (x - high.astype(jnp.float32)).astype(jnp.bfloat16)


def window_rows(filt, wave_ref):
    flipped = jnp.transpose(filt)
    real = jnp.zeros((32, 128), jnp.float32)
    imag = jnp.zeros((32, 128), jnp.float32)
    for a in range(32):
        r, q = a // 4, a % 4
        column = jnp.broadcast_to(flipped[32 * q : 32 * q + 32, r : r + 1], (32, 128))
        real = real + column * wave_ref[a : a + 1, :128]
        imag = imag + column * wave_ref[32 + a : 33 + a, :128]
    rows = []
    for m in range(8):
        lanes = pl.ds(128 * (m + 1), 128)
        value = real * wave_ref[0:32, lanes] - imag * wave_ref[32:64, lanes]
        rows.append(jnp.sum(value, axis=0, keepdims=True))
    return rows


def build_circulant(rows, store):
    lane = lax.broadcasted_iota(jnp.int32, (128, 128), 1)
    down = lax.broadcasted_iota(jnp.int32, (128, 128), 0)
    shift = lax.rem(lane - down + 128, 128)
    upper = lane >= down
    rolled = []
    for m in range(8):
        row = jnp.broadcast_to(rows[m], (8, 128))
        rolled.append(
            jnp.concatenate(
                [
                    jnp.take_along_axis(row, shift[8 * g : 8 * g + 8], axis=1, mode="promise_in_bounds")
                    for g in range(16)
                ],
                axis=0,
            )
        )
    blocks = [jnp.where(upper, rolled[(-d) % 8], rolled[(-d - 1) % 8]) for d in range(8)]
    for d in range(-3, 4):
        near, far = blocks[d % 8], blocks[(d + 4) % 8]
        for sign, value in enumerate((0.5 * (near + far), 0.5 * (near - far))):
            for i in range(4):
                j = i - d
                if 0 <= j < 4:
                    store(sign, i, j, value)


def dot3(a, b):
    d = functools.partial(jnp.dot, preferred_element_type=jnp.float32)
    return d(a[0], b[0]) + d(a[0], b[1]) + d(a[1], b[0])


def fused_kernel(
    field_hbm, bins_hbm, rate_hbm, mask_hbm, route_hbm, fx_hbm, fy_hbm, wave_hbm,
    recomb_ref, smooth_ref, share_ref,
    field_buf, lt_ref, rt_ref, zsend_ref, recv_ref, mx_ref, my_ref, mid_ref, send_ref, back_ref, give_ref,
    bins_ref, rate_ref, mask_tiles, route_tiles, fx_ref, fy_ref, wave_ref, wide_ref, table_ref, mask_ref, route_ref, coef_ref, sum_ref,
    in_sem, small_sem, fsend_sem, frecv_sem, bsend_sem, brecv_sem, lsend_sem, lrecv_sem,
):
    n_gx, n_gy = lax.axis_size("gx"), lax.axis_size("gy")
    total = n_gx * n_gy
    gx, gy = lax.axis_index("gx"), lax.axis_index("gy")
    me = gx * n_gy + gy
    cx, core = gx // 2, lax.rem(gx, 2)
    cy, cz = gy // 4, lax.rem(gy, 4)
    layers = bins_ref.shape[1]
    chunks = zsend_ref.shape[0]
    pieces = send_ref.shape[0]
    tile = lax.rem(cx + cy + cz, 4)
    plane = tile * EDGE + gx * 4 + cy
    xs = [lax.rem(cx + e, 4) for e in range(4)]
    ys = [lax.rem(cy + b, 4) for b in range(4)]
    tys = [lax.rem(gy + j, n_gy) for j in range(n_gy)]

    def fetch(c, slot):
        return pltpu.make_async_copy(
            field_hbm.at[:, pl.ds(pl.multiple_of(c * 8, 8), 8), :], field_buf.at[slot], in_sem.at[slot]
        )

    small = [
        pltpu.make_async_copy(source, target, small_sem.at[i])
        for i, (source, target) in enumerate(
            (
                (rate_hbm, rate_ref), (mask_hbm, mask_tiles), (bins_hbm, bins_ref),
                (route_hbm, route_tiles), (fx_hbm, fx_ref), (fy_hbm, fy_ref), (wave_hbm, wave_ref),
            )
        )
    ]
    fetch(0, 0).start()
    for copy in small:
        copy.start()
    barrier = pltpu.get_barrier_semaphore()

    def greet(i, _):
        tx = lax.rem(gx + i, n_gx)
        for j in range(1, n_gy):
            pl.semaphore_signal(barrier, inc=1, device_id=(tx, tys[j]), device_id_type=MESH)

        @pl.when(i > 0)
        def _():
            pl.semaphore_signal(barrier, inc=1, device_id=(tx, gy), device_id_type=MESH)

        return 0

    lax.fori_loop(0, n_gx, greet, 0)
    small[0].wait()
    build_pair_table(rate_ref, wide_ref, table_ref)
    small[1].wait()
    build_rows(mask_tiles, mask_ref)
    small[2].wait()
    sum_ref[...] = jnp.zeros_like(sum_ref)

    def forward(c, t, side, zs, e, b):
        tx = xs[e] * 2 + side
        ty = ys[b] * 4 + zs[(e + b) % 4]
        return pltpu.make_async_remote_copy(
            src_ref=zsend_ref.at[c, t * EDGE + tx * 4 + ys[b]], dst_ref=recv_ref.at[c, me],
            send_sem=fsend_sem.at[c], recv_sem=frecv_sem.at[c],
            device_id=(tx, ty), device_id_type=MESH,
        )

    def send_unit(c, t, half):
        zs = [lax.rem(t - cx - cy - m + 16, 4) for m in range(4)]
        side = lax.rem(core + half, 2)
        for e in range(4):
            for b in range(4):
                if e + b > 0:
                    forward(c, t, side, zs, e, b).start()

        @pl.when(jnp.logical_or(half > 0, t != tile))
        def _():
            forward(c, t, side, zs, 0, 0).start()

    def evaluate_unit(u, sending):
        c = u // layers
        t = lax.rem(u, layers)
        slot = lax.rem(c, 2)
        band = c * 8 // EDGE
        before = u - 1

        @pl.when(t == 0)
        def _():
            @pl.when(c + 1 < chunks)
            def _():
                fetch(c + 1, 1 - slot).start()

            fetch(c, slot).wait()
            field2 = field_buf.at[slot].reshape(128 * 8, 128)
            for y in range(8):
                lt_ref[y] = field2[pl.ds(y, 128, stride=8), :].T

        zsend2 = zsend_ref.at[c].reshape(128 * 8, 128)
        z = pl.ds(pl.multiple_of(EDGE * t, EDGE), EDGE)
        row = band * layers + t

        def half_rows(half, _):
            if sending:
                send_unit(before // layers, lax.rem(before, layers), half)
            sums = jnp.zeros((8, 128), jnp.float32)
            mask = (mask_ref[pl.ds(row, 1), :] == 1).astype(jnp.float32)
            for i in range(4):
                y = half * 4 + i
                value = column_integral(
                    lt_ref[y, z, :], bins_ref[c * 8 + y, pl.ds(t, 1), :], table_ref, coef_ref.at[i]
                )
                value = value * mask
                rt_ref[y, z, :] = value
                zsend2[pl.ds(t * EDGE * 8 + y, EDGE, stride=8), :] = value
                sums = sums + ((value[0:8] + value[8:16]) + (value[16:24] + value[24:32]))
            sum_ref[row] += sums
            return 0

        lax.fori_loop(0, 2, half_rows, 0)

        @pl.when(t == layers - 1)
        def _():
            out2 = recomb_ref.at[c].reshape(128 * 8, 128)
            for y in range(8):
                out2[pl.ds(y, 128, stride=8), :] = rt_ref[y].T
            recv_ref[c, me] = zsend_ref[c, plane]

    evaluate_unit(0, False)
    pl.semaphore_wait(barrier, total - 1)

    def later_unit(u, _):
        evaluate_unit(u, True)
        return 0

    lax.fori_loop(1, chunks * layers, later_unit, 0)

    def last_unit(half, _):
        send_unit(chunks - 1, layers - 1, half)
        return 0

    lax.fori_loop(0, 2, last_unit, 0)

    small[3].wait()
    build_rows(route_tiles, route_ref)
    flat = jnp.concatenate(
        [jnp.sum(sum_ref[i], axis=0, keepdims=True) for i in range(8)], axis=0
    )
    for g in range(16):
        give_ref[g] = jnp.where(route_ref[...] == g, flat, 0.0)
    share_ref[gy] = give_ref[gy]

    for copy in small[4:]:
        copy.wait()

    def store_x(sign, i, j, value):
        for part, piece in enumerate(split(value)):
            mx_ref[sign, part, pl.ds(128 * i, 128), pl.ds(128 * j, 128)] = piece

    def store_y(sign, i, j, value):
        order = jnp.concatenate(
            [value[64 * h + 8 * p : 64 * h + 8 * p + 8] for p in range(8) for h in range(2)], axis=0
        )
        for part, piece in enumerate(split(order)):
            for p in range(8):
                my_ref[sign, part, p, pl.ds(16 * i, 16), pl.ds(128 * j, 128)] = piece[16 * p : 16 * p + 16]

    build_circulant(window_rows(fx_ref[...], wave_ref), store_x)
    build_circulant(window_rows(fy_ref[...], wave_ref), store_y)

    def load_copy(k):
        ty = lax.rem(gy + k, n_gy)
        return pltpu.make_async_remote_copy(
            src_ref=give_ref.at[ty], dst_ref=share_ref.at[gy],
            send_sem=lsend_sem, recv_sem=lrecv_sem,
            device_id=(gx, ty), device_id_type=MESH,
        )

    def load_send(k, _):
        load_copy(k).start()
        return 0

    lax.fori_loop(1, n_gy, load_send, 0)

    def wait_all(ref, send_sem, recv_sem, what):
        copy = pltpu.make_async_remote_copy(
            src_ref=ref, dst_ref=ref, send_sem=send_sem, recv_sem=recv_sem,
            device_id=(gx, gy), device_id_type=MESH,
        )
        copy.wait_recv() if what == "recv" else copy.wait_send()

    def first(c, _):
        for q in range(2):
            wait_all(recv_ref.at[2 * c + q, pl.ds(0, total - 1)], fsend_sem.at[2 * c + q], frecv_sem.at[2 * c + q], "recv")

        def rows(i, j0):
            src = pl.ds(i * 16 + j0, 8)
            return jnp.concatenate([recv_ref[2 * c, src], recv_ref[2 * c + 1, src]], axis=1).reshape(128, 128)

        for ysign in range(2):
            parts = [[], []]
            for i in range(4):
                a0, a1 = rows(i, 0), rows(i, 8)
                b0, b1 = rows(i + 4, 0), rows(i + 4, 8)
                if ysign == 0:
                    a, b = a0 + a1, b0 + b1
                else:
                    a, b = a0 - a1, b0 - b1
                parts[0].append(a + b)
                parts[1].append(a - b)
            for xsign in range(2):
                value = split(jnp.concatenate(parts[xsign], axis=1))
                out = split(dot3(value, (mx_ref[xsign, 0], mx_ref[xsign, 1])))
                for part in range(2):
                    for j in range(8):
                        mid_ref[ysign, part, pl.ds(pl.multiple_of(64 * j + 16 * c, 16), 16), pl.ds(512 * xsign, 512)] = out[part][16 * j : 16 * j + 16]
        return 0

    lax.fori_loop(0, chunks // 2, first, 0)

    def backward(p, tx, ty):
        return pltpu.make_async_remote_copy(
            src_ref=send_ref.at[p, tx * n_gy + ty], dst_ref=back_ref.at[p, plane],
            send_sem=bsend_sem.at[p], recv_sem=brecv_sem.at[p],
            device_id=(tx, ty), device_id_type=MESH,
        )

    def second(p, _):
        res = [
            dot3((my_ref[ysign, 0, p], my_ref[ysign, 1, p]), (mid_ref[ysign, 0], mid_ref[ysign, 1]))
            for ysign in range(2)
        ]
        for yh in range(2):
            both = res[0] + res[1] if yh == 0 else res[0] - res[1]
            plus, minus = both[:, :512], both[:, 512:]
            for xh in range(2):
                value = plus + minus if xh == 0 else plus - minus
                for i in range(4):
                    for j in range(8):
                        send_ref[p, (xh * 4 + i) * 16 + yh * 8 + j] = value[8 * j : 8 * j + 8, 128 * i : 128 * i + 128]
        back_ref[p, plane] = send_ref[p, me]

        def send(i, _):
            for j in range(1, n_gy):
                backward(p, lax.rem(gx + i + 3 * j, n_gx), tys[j]).start()

            @pl.when(i > 0)
            def _():
                backward(p, lax.rem(gx + i, n_gx), gy).start()

            return 0

        lax.fori_loop(0, n_gx, send, 0)
        return 0

    lax.fori_loop(0, pieces, second, 0)

    def finish_forward(c, _):
        wait_all(zsend_ref.at[c, pl.ds(0, total - 1)], fsend_sem.at[c], frecv_sem.at[c], "send")
        return 0

    lax.fori_loop(0, chunks, finish_forward, 0)
    wait_all(share_ref.at[pl.ds(0, n_gy - 1)], lsend_sem, lrecv_sem, "recv")
    wait_all(give_ref.at[pl.ds(0, n_gy - 1)], lsend_sem, lrecv_sem, "send")

    def finish_backward(p, _):
        wait_all(back_ref.at[p, pl.ds(0, total - 1)], bsend_sem.at[p], brecv_sem.at[p], "recv")
        source = back_ref.at[p].reshape(128 * 8, 128)
        target = smooth_ref.at[p].reshape(128 * 8, 128)
        for y in range(8):
            target[pl.ds(y, 128, stride=8), :] = source[pl.ds(y, 128, stride=8), :].T
        wait_all(send_ref.at[p, pl.ds(0, total - 1)], bsend_sem.at[p], brecv_sem.at[p], "send")
        return 0

    lax.fori_loop(0, pieces, finish_backward, 0)


def fused_call(log_crit, bins, rate, tile_mask, tile_route, fx, fy):
    f32, bf16, i32 = jnp.float32, jnp.bfloat16, jnp.int32
    cells_x, cells_y, depth = log_crit.shape
    total = lax.axis_size("gx") * lax.axis_size("gy")
    chunks = cells_y // 8
    waves = wave_tables(fx.size)
    dma = pltpu.SemaphoreType.DMA
    vmem, hbm = pl.BlockSpec(memory_space=VMEM), pl.BlockSpec(memory_space=pltpu.HBM)
    blocks = jax.ShapeDtypeStruct((chunks, cells_x, 8, depth), f32)
    return pl.pallas_call(
        fused_kernel,
        in_specs=[hbm] * 8,
        out_specs=[vmem, vmem, vmem],
        out_shape=[blocks, blocks, jax.ShapeDtypeStruct((16, 8, 128), f32)],
        scratch_shapes=[
            VMEM((2, cells_x, 8, depth), f32),
            VMEM((8, 128, 128), f32),
            VMEM((8, 128, 128), f32),
            VMEM((chunks, total, 8, 128), f32),
            VMEM((chunks, total, 8, 128), f32),
            VMEM((2, 2, 512, 512), bf16),
            VMEM((2, 2, 8, 64, 512), bf16),
            VMEM((2, 2, 512, 1024), bf16),
            VMEM((chunks, total, 8, 128), f32),
            VMEM((chunks, total, 8, 128), f32),
            VMEM((16, 8, 128), f32),
            VMEM(bins.shape, i32),
            VMEM(rate.shape, bf16),
            VMEM(tile_mask.shape, i32),
            VMEM(tile_route.shape, i32),
            VMEM(fx.shape, f32),
            VMEM(fy.shape, f32),
            VMEM(waves.shape, f32),
            VMEM(rate.shape, f32),
            VMEM(rate.shape, f32),
            VMEM((8, 128), i32),
            VMEM((8, 128), i32),
            VMEM((4, *rate.shape), f32),
            VMEM((8, 8, 128), f32),
            dma((2,)), dma((7,)), dma((chunks,)), dma((chunks,)), dma((chunks,)), dma((chunks,)), dma, dma,
        ],
        compiler_params=pltpu.CompilerParams(
            vmem_limit_bytes=40 * 2**20, collective_id=0, has_side_effects=True
        ),
        name="fused",
    )(*(pltpu.with_memory_space_constraint(a, pltpu.HBM) for a in (log_crit, bins, rate, tile_mask, tile_route, fx, fy, jnp.asarray(waves))))


def final_kernel(recomb_ref, smooth_ref, share_ref, recomb_hbm, smooth_hbm, load_ref, sems):
    copies = []
    for a, (source, target) in enumerate(((recomb_ref, recomb_hbm), (smooth_ref, smooth_hbm))):
        for c in range(source.shape[0]):
            copies.append(pltpu.make_async_copy(source.at[c], target.at[:, pl.ds(8 * c, 8), :], sems.at[a, c]))
    for copy in copies:
        copy.start()
    shares = jnp.sum(share_ref[...], axis=0)
    load_ref[...] = jnp.sum(jnp.sum(shares, axis=0, keepdims=True), axis=1, keepdims=True) * (2.0**-19)
    for copy in copies:
        copy.wait()


def final_call(recomb, smooth, share):
    chunks, cells_x, rows, depth = recomb.shape
    f32 = jnp.float32
    whole = jax.ShapeDtypeStruct((cells_x, chunks * rows, depth), f32)
    vmem, anywhere = pl.BlockSpec(memory_space=VMEM), pl.BlockSpec(memory_space=pl.ANY)
    return pl.pallas_call(
        final_kernel,
        in_specs=[vmem] * 3,
        out_specs=[anywhere, anywhere, vmem],
        out_shape=[whole, whole, jax.ShapeDtypeStruct((1, 1), f32)],
        scratch_shapes=[pltpu.SemaphoreType.DMA((2, chunks))],
        compiler_params=pltpu.CompilerParams(vmem_limit_bytes=16 * 2**20),
        name="final",
    )(recomb, smooth, share)


def on_device(log_crit, col_bins, rate_table, tile_mask, tile_route, filt_x, filt_y):
    recomb, smooth, share = fused_call(
        log_crit, col_bins.transpose(1, 2, 0), rate_table.T, tile_mask, tile_route,
        filt_x.reshape(-1, 128), filt_y.reshape(-1, 128),
    )
    recomb, smooth, load = final_call(recomb, smooth, share)
    return recomb, smooth, load


def solution(mesh):
    block = P("gx", "gy", None)
    return jax.shard_map(
        on_device,
        mesh=mesh,
        in_specs=(block, block, P(), block, block, P(), P()),
        out_specs=(block, block, P("gx", "gy")),
        check_vma=False,
    )
```

time: 152 us -> 122 us (0.80)
  Pallas kernels: 137 us -> 121 us
  local copies, waits for them, and re-layouts: 5.52 us -> 0 us
  other arithmetic: 4.2 us -> 0 us
  matrix products: 3.71 us -> 0 us
    pallas_call x2, Pallas kernels: 137 us -> 121 us  [the longest x1 117 us: fused_call(): pl.pallas_call(fused_kernel, in_specs=[hbm] * 8, out_specs=[vmem, vmem, v...]
    reshape x6 -> x0, local copies, waits for them, and re-layouts: 3.74 us -> none  [the longest x2 1.51 us: kernel_rows(): grid = filt.reshape(outer, inner)]
    dot_general x4 -> x0, matrix products: 3.71 us -> none  [the longest x2 1.86 us: kernel_rows(): imag = dot('ab,ar->br', grid, jnp.asarray(np.sin(small), jnp.float32))]
where the time goes in v1:
time: 122 us; the launch traced here: 121 us
  Pallas kernels  121 us (99%)
    pallas_call x1, Pallas kernels, fused_call(): pl.pallas_call(fused_kernel, in_specs=[hbm] * 8, out_specs=[vmem, vmem, v...  117 us
    pallas_call x1, Pallas kernels, final_call(): pl.pallas_call(final_kernel, in_specs=[vmem] * 3, out_specs=[anywhere, an...  3.93 us

profile of v1, /device:TPU:1, one launch (start us, length us, event | category | flops | bytes accessed | tf_op | source)
XLA Modules:
  0.0 121.4 jit_solution(2189264018585577801)
XLA Ops:
  0.6 116.9 %fused.1 = (f32[8,128,8,128]{3,2,1,0:T(8,128)S(1)}, f32[8,128,8,128]{3,2,1,0:T(8,128)S(1)}, f32[16,8,128]{2,1,0:T(8,128)S(1)}) custom-call(f32[128,64,128]{2,1,0:T(8,128)} %field_hbm.1, s32[64,4,128]{2,1,0:T(4,128)} %bitcast.4, bf16[64,128]{1,0:T(8,128)(2,1)} %bitcast.5, s32[4,2,4]{2,1,0:T(2,128)} %mask_hbm.1, s32[4,2,4]{2,1,0:T(2,128)} %route_hbm.1, ...), custom_call_target="tpu_custom_call" | custom-call | tf_op jit(solution)/shard_map/fused/pallas_call | solution.py:421
  117.5 3.9 %final.1 = (f32[128,64,128]{2,1,0:T(8,128)}, f32[128,64,128]{2,1,0:T(8,128)}, f32[1,1]{1,0:T(1,128)}) custom-call(f32[8,128,8,128]{3,2,1,0:T(8,128)S(1)} %get-tuple-element.6.recomb_ref, f32[8,128,8,128]{3,2,1,0:T(8,128)S(1)} %get-tuple-element.7.smooth_ref, f32[16,8,128]{2,1,0:T(8,128)S(1)} %get-tuple-element.8.share_ref), custom_call_target="tpu_custom_call" | custom-call | tf_op jit(solution)/shard_map/final/pallas_call | solution.py:478
